TPU v7x, 16 devices: a 4x2x1 block of a 4x4x8 slice. The times are simulated.
16 devices in a mesh: dp: 2 (over y, z), tp: 8 (over x, core).
Axes of the slice: x: 4, y: 2, z: 1, core: 2. Of those that a mesh axis runs over, the one named last changes fastest.
The devices are a block of a 4x4x8 slice.
Arguments:
- x_in: bfloat16 [256, 4096], P('dp'), parts along dimension 0
- tok_pos: int32 [256], P('dp'), parts along dimension 0
- self_k: bfloat16 [256, 64, 16, 256], P('dp', None, 'tp'), parts along dimension 0
- self_v: bfloat16 [256, 64, 16, 256], P('dp', None, 'tp'), parts along dimension 0
- cross_k: bfloat16 [256, 64, 16, 256], P('dp', None, 'tp'), parts along dimension 0
- cross_v: bfloat16 [256, 64, 16, 256], P('dp', None, 'tp'), parts along dimension 0
- enc_mask: int32 [256, 64], P('dp'), parts along dimension 0
- rel_bias: float32 [32, 16], P(None, 'tp')
- w_q: bfloat16 [4096, 4096], P(None, 'tp')
- w_k: bfloat16 [4096, 4096], P(None, 'tp')
- w_v: bfloat16 [4096, 4096], P(None, 'tp')
- w_o: bfloat16 [4096, 4096], P('tp')
- cross_q: bfloat16 [4096, 4096], P(None, 'tp')
- cross_o: bfloat16 [4096, 4096], P('tp')
- w_gate: bfloat16 [4096, 16384], P(None, 'tp')
- w_up: bfloat16 [4096, 16384], P(None, 'tp')
- w_down: bfloat16 [16384, 4096], P('tp')
- norm_self: bfloat16 [4096], replicated
- norm_cross: bfloat16 [4096], replicated
- norm_mlp: bfloat16 [4096], replicated
Outputs:
- output 1: bfloat16 [256, 4096], P('dp'), parts along dimension 0
- output 2: bfloat16 [256, 64, 16, 256], P('dp', None, 'tp'), parts along dimension 0
- output 3: bfloat16 [256, 64, 16, 256], P('dp', None, 'tp'), parts along dimension 0
There are 2 independent parts. A program takes and returns all parts, laid end to end along the dimension named above; an argument that names none is the same for every part.
All inputs are finite; a program needn't handle non-finite values.
Results may differ from a plain program's by a relative error of at most 0.0187279.
Values are sent between devices in bfloat16 or wider.
A program may use at most 768 MiB of HBM per device.

v0:
```python
import math
import jax
import jax.numpy as jnp
from jax import lax
from jax.sharding import PartitionSpec as P

BUCKET_EDGES = tuple(int(math.ceil(16.0 * 8.0 ** (bucket_step / 16.0))) for bucket_step in range(1, 16))
NEG_FILL = -1e30


def rms_norm(values, norm_scale):
    inv_rms = lax.rsqrt(jnp.mean(values * values, axis=-1, keepdims=True) + 1e-6)
    return (values * inv_rms * norm_scale.astype(jnp.float32)).astype(jnp.bfloat16)


def project(normed, weight):
    return jnp.dot(normed, weight, preferred_element_type=jnp.float32).astype(jnp.bfloat16)


def rel_bucket(distance):
    bucket_edges = jnp.array(BUCKET_EDGES, dtype=jnp.int32)
    far_bucket = 16 + jnp.sum((distance[..., None] >= bucket_edges).astype(jnp.int32), axis=-1)
    return jnp.where(distance < 16, distance, far_bucket)


def attend(queries, keys_all, values_all, extra):
    scores = jnp.einsum('bhk,bthk->bht', queries, keys_all, preferred_element_type=jnp.float32) + extra
    probs_bf = jax.nn.softmax(scores, axis=-1).astype(jnp.bfloat16)
    mixed_out = jnp.einsum('bht,bthk->bhk', probs_bf, values_all, preferred_element_type=jnp.float32)
    return mixed_out.astype(jnp.bfloat16)


def self_terms(tok_pos, rel_bias, t_len):
    key_index = jnp.arange(t_len)
    at_pos = (key_index[None, :] == tok_pos[:, None])[:, :, None, None]
    distance = jnp.maximum(tok_pos[:, None] - key_index[None, :], 0)
    bias_rows = jnp.swapaxes(jnp.take(rel_bias, rel_bucket(distance), axis=0), 1, 2)
    causal = (key_index[None, :] <= tok_pos[:, None])[:, None, :]
    return at_pos, jnp.where(causal, bias_rows, NEG_FILL)


def solution(mesh):
    def tp_sum(partial_out):
        return lax.psum(partial_out.astype(jnp.bfloat16), 'tp').astype(jnp.float32)

    def local_layer(x_in, tok_pos, self_k, self_v, cross_k, cross_v, enc_mask, rel_bias, w_q, w_k, w_v, w_o, cross_q, cross_o, w_gate, w_up, w_down, norm_self, norm_cross, norm_mlp):
        row_count, t_len, head_count, head_dim = self_k.shape
        head_shape = (row_count, head_count, head_dim)
        flat_dim = head_count * head_dim
        residual = x_in.astype(jnp.float32)
        normed = rms_norm(residual, norm_self)
        queries = project(normed, w_q).reshape(head_shape)
        new_keys = project(normed, w_k).reshape(head_shape)
        new_values = project(normed, w_v).reshape(head_shape)
        at_pos, self_extra = self_terms(tok_pos, rel_bias, t_len)
        new_self_k = jnp.where(at_pos, new_keys[:, None], self_k)
        new_self_v = jnp.where(at_pos, new_values[:, None], self_v)
        mixed_self = attend(queries, new_self_k, new_self_v, self_extra)
        residual = residual + tp_sum(jnp.dot(mixed_self.reshape(row_count, flat_dim), w_o, preferred_element_type=jnp.float32))
        normed = rms_norm(residual, norm_cross)
        cross_queries = project(normed, cross_q).reshape(head_shape)
        cross_extra = jnp.where(enc_mask[:, None, :] != 0, 0.0, NEG_FILL)
        mixed_cross = attend(cross_queries, cross_k, cross_v, cross_extra)
        residual = residual + tp_sum(jnp.dot(mixed_cross.reshape(row_count, flat_dim), cross_o, preferred_element_type=jnp.float32))
        normed = rms_norm(residual, norm_mlp)
        gate_pre = jnp.dot(normed, w_gate, preferred_element_type=jnp.float32)
        up_pre = jnp.dot(normed, w_up, preferred_element_type=jnp.float32)
        hidden = (jax.nn.gelu(gate_pre, approximate=True) * up_pre).astype(jnp.bfloat16)
        residual = residual + tp_sum(jnp.dot(hidden, w_down, preferred_element_type=jnp.float32))
        return residual.astype(jnp.bfloat16), new_self_k, new_self_v

    cache_spec = P('dp', None, 'tp', None)
    split_cols = P(None, 'tp')
    split_rows = P('tp', None)
    in_specs = (P('dp', None), P('dp'), cache_spec, cache_spec, cache_spec, cache_spec, P('dp', None), split_cols, split_cols, split_cols, split_cols, split_rows, split_cols, split_rows, split_cols, split_cols, split_rows, P(None), P(None), P(None))
    out_specs = (P('dp', None), cache_spec, cache_spec)
    return jax.shard_map(local_layer, mesh=mesh, in_specs=in_specs, out_specs=out_specs, check_vma=False)
```

profile of v0, /device:TPU:113, one launch (start us, length us, event | category | flops | bytes accessed | tf_op | source)
XLA Modules:
  0.0 313.4 jit_solution(16232536120636632134)
XLA Ops:
  7.3 0.7 subtract_maximum_fusion
  8.0 0.8 convert_reduce_fusion
  8.8 0.7 iota_compare_fusion
  9.5 0.7 compare_select_fusion
  10.1 0.7 convert_element_type.73
  10.8 1.5 fusion.13
  12.4 3.3 %convolution_convert_fusion.5 = bf16[128,512]{1,0:T(8,128)(2,1)S(1)} fusion(bf16[4096,512]{1,0:T(8,128)(2,1)} %param.30, bf16[128,4096]{1,0:T(8,128)(2,1)} %param.21, f32[4096]{0:T(1024)S(1)} %convert_element_type.73, f32[128]{0:T(128)S(1)} %add_rsqrt_fusion.2), kind=kOutput, calls=%fused_computation.40 | convolution fusion | flops 539033600 | bytes 5390848 | tf_op jit(solution)/shard_map/dot_general | solution.py:17
  15.7 2.9 convolution_convert_fusion.4
  18.8 3.0 convolution_convert_fusion.6
  21.9 21.6 %broadcast_select_fusion = (bf16[128,64,2,256]{3,2,1,0:T(2,128)(2,1)}, bf16[128,64,2,256]{3,2,1,0:T(2,128)(2,1)S(1)}) fusion(bf16[128,64,2,256]{3,2,1,0:T(2,128)(2,1)} %param.24, pred[128,64]{1,0:T(8,128)(4,1)S(1)} %copy.37, bf16[128,2,256]{2,1,0:T(2,128)(2,1)S(1)} %broadcast_in_dim.86, bf16[128,64,2,256]{3,2,1,0:T(2,128)(2,1)} %param.23, ...), kind=kLoop, calls=%fused_computation.5 | loop fusion | flops 8388608 | bytes 33824768 | tf_op jit(solution)/shard_map/jit(_where)/select_n | solution.py:57
  43.5 3.4 %copy-done.2 = bf16[128,64,2,256]{3,2,1,0:T(2,128)(2,1)} copy-done((bf16[128,64,2,256]{3,2,1,0:T(2,128)(2,1)}, bf16[128,64,2,256]{3,2,1,0:T(2,128)(2,1)S(1)}, u32[]{:S(2)}) %copy-start.2) | copy-done | bytes 8388632
  46.9 2.3 fusion.10
  49.1 2.7 copy.44
  52.4 27.7 %gather_fusion = f32[8192,2]{1,0:T(8,128)} fusion(f32[32,2]{1,0:T(8,128)S(1)} %copy.41, s32[8192]{0:T(1024)S(1)} %broadcast_clamp_fusion), kind=kCustom, calls=%fused_computation | custom fusion | bytes 163840 | tf_op jit(solution)/shard_map/jit(_take)/gather | solution.py:37
  80.1 5.3 %fusion.16 = bf16[128,2,64,1]{1,2,0,3:T(8,128)(2,1)S(1)} fusion(f32[128,2,1,64]{1,3,0,2:T(8,128)} %copy.44, f32[128,64,2]{2,1,0:T(8,128)} %bitcast.57, pred[128,64]{1,0:T(8,128)(4,1)S(1)} %copy.39, pred[128,64]{1,0:T(8,128)(4,1)S(1)} %copy.38), kind=kOutput, calls=%fused_computation.35 | output fusion | flops 98942 | bytes 180224 | tf_op jit(solution)/shard_map/div | solution.py:28
  85.4 1.8 copy.45
  87.3 4.7 %fusion.8 = bf16[128,2,1,256]{3,2,1,0:T(2,128)(2,1)S(1)} fusion(bf16[128,2,64,1]{2,3,1,0:T(2,128)(2,1)S(1)} %copy.45, bf16[128,64,2,256]{3,2,1,0:T(2,128)(2,1)} %get-tuple-element.3), kind=kOutput, calls=%fused_computation.11 | convolution fusion | flops 8388608 | bytes 8552448 | tf_op jit(solution)/shard_map/bht,bthk->bhk/dot_general | solution.py:29
  92.2 1.7 convolution_convert_fusion.2
  93.9 0.2 all-reduce.6.cloned.1.call-start
  94.2 55.0 %all-reduce.4.cloned.1.call-done = bf16[128,4096]{1,0:T(8,128)(2,1)} async-done(((bf16[128,4096]{1,0:T(8,128)(2,1)}), bf16[128,4096]{1,0:T(8,128)(2,1)}) %all-reduce.4.cloned.1.call-update) | async-done | bytes 1048592 | tf_op jit(solution)/shard_map/psum | solution.py:44
  149.2 1.6 multiply_reduce_fusion.1
  150.9 3.3 %convolution_convert_fusion.3 = bf16[128,512]{1,0:T(8,128)(2,1)S(1)} fusion(bf16[4096,512]{1,0:T(8,128)(2,1)} %param.33, bf16[128,4096]{1,0:T(8,128)(2,1)} %all-reduce.4.cloned.1.call-done, bf16[128,4096]{1,0:T(8,128)(2,1)S(1)} %copy-done, f32[4096]{0:T(1024)S(1)} %convert_element_type.83, f32[128]{0:T(128)S(1)} %add_rsqrt_fusion.1), kind=kOutput, calls=%fused_computation.38 | convolution fusion | flops 540082176 | bytes 6439424 | tf_op jit(solution)/shard_map/dot_general | solution.py:17
  154.3 5.6 %fusion.6 = f32[128,2,1,64]{3,2,1,0:T(1,128)S(1)} fusion(bf16[128,2,256,1]{2,3,1,0:T(2,128)(2,1)S(1)} %reshape.205, bf16[128,64,2,256]{3,2,1,0:T(2,128)(2,1)} %param.25), kind=kOutput, calls=%fused_computation.9 | convolution fusion | flops 8388608 | bytes 8585216 | tf_op jit(solution)/shard_map/bhk,bthk->bht/dot_general | solution.py:27
  160.2 4.7 %fusion.4 = bf16[128,2,1,256]{3,2,1,0:T(2,128)(2,1)S(1)} fusion(bf16[128,2,64,1]{2,3,1,0:T(2,128)(2,1)S(1)} %copy.51, bf16[128,64,2,256]{3,2,1,0:T(2,128)(2,1)} %param.26), kind=kOutput, calls=%fused_computation.7 | convolution fusion | flops 8388608 | bytes 8552448 | tf_op jit(solution)/shard_map/bht,bthk->bhk/dot_general | solution.py:29
  165.1 1.7 convolution_convert_fusion.1
  167.0 53.6 %all-reduce.6.cloned.1.call-done = bf16[128,4096]{1,0:T(8,128)(2,1)} async-done(((bf16[128,4096]{1,0:T(8,128)(2,1)}), bf16[128,4096]{1,0:T(8,128)(2,1)}) %all-reduce.6.cloned.1.call-update) | async-done | bytes 1048592 | tf_op jit(solution)/shard_map/psum | solution.py:44
  220.6 1.8 multiply_reduce_fusion
  222.4 1.8 multiply_convert_fusion
  224.2 9.1 %fusion.47 = f32[128,2048]{1,0:T(8,128)} fusion(bf16[128,4096]{1,0:T(8,128)(2,1)S(1)} %multiply_convert_fusion, bf16[4096,2048]{1,0:T(8,128)(2,1)} %param.35), kind=kOutput, calls=%fused_computation.85 | convolution fusion | flops 2147483648 | bytes 18874368 | tf_op jit(solution)/shard_map/dot_general | solution.py:66
  233.2 16.7 %convolution_convert_fusion = bf16[128,4096]{1,0:T(8,128)(2,1)} fusion(bf16[2048,4096]{1,0:T(8,128)(2,1)} %param.37, bf16[128,4096]{1,0:T(8,128)(2,1)S(1)} %multiply_convert_fusion, bf16[4096,2048]{1,0:T(8,128)(2,1)} %param.36, f32[128,2048]{1,0:T(8,128)} %fusion.47), kind=kOutput, calls=%fused_computation.15 | convolution fusion | flops 4298113024 | bytes 36700160 | tf_op jit(solution)/shard_map/dot_general | solution.py:69
  250.0 53.7 %all-reduce.8.cloned.1.call-done = bf16[128,4096]{1,0:T(8,128)(2,1)} async-done(((bf16[128,4096]{1,0:T(8,128)(2,1)}), bf16[128,4096]{1,0:T(8,128)(2,1)}) %all-reduce.8.cloned.1.call-update) | async-done | bytes 1048592 | tf_op jit(solution)/shard_map/psum | solution.py:44
  303.7 3.2 %add_convert_fusion = bf16[128,4096]{1,0:T(8,128)(2,1)} fusion(bf16[128,4096]{1,0:T(8,128)(2,1)} %all-reduce.8.cloned.1.call-done, bf16[128,4096]{1,0:T(8,128)(2,1)} %all-reduce.6.cloned.1.call-done, bf16[128,4096]{1,0:T(8,128)(2,1)S(1)} %copy-done.1, bf16[128,4096]{1,0:T(8,128)(2,1)S(1)} %copy-done), kind=kLoop, calls=%fused_computation.29 | loop fusion | flops 4194304 | bytes 5242880 | tf_op jit(solution)/shard_map/convert_element_type | solution.py:70
  (46 shorter events, 1.8 us)
Async XLA Ops:
  7.2 8.5 %copy-start = (bf16[128,4096]{1,0:T(8,128)(2,1)S(1)}, bf16[128,4096]{1,0:T(8,128)(2,1)}, u32[]{:S(2)}) copy-start(bf16[128,4096]{1,0:T(8,128)(2,1)} %param.21) | copy-start | bytes 3145732
  7.2 142.1 %all-reduce.4.cloned.1.call-start = ((), (), s32[]{:S(2)}) async-start(), calls=%async_computation | async-start | bytes 2097152 | tf_op jit(solution)/shard_map/psum | solution.py:44
  43.5 3.4 %copy-start.2 = (bf16[128,64,2,256]{3,2,1,0:T(2,128)(2,1)}, bf16[128,64,2,256]{3,2,1,0:T(2,128)(2,1)S(1)}, u32[]{:S(2)}) copy-start(bf16[128,64,2,256]{3,2,1,0:T(2,128)(2,1)S(1)} %get-tuple-element.4) | copy-start | bytes 25165828
  49.1 3.2 %copy-start.8 = (f32[32,2]{0,1:T(2,128)S(1)}, f32[32,2]{0,1:T(2,128)}, u32[]{:S(2)}) copy-start(f32[32,2]{0,1:T(2,128)} %param.28) | copy-start | bytes 772
  87.2 4.9 %copy-start.3 = (bf16[512,4096]{1,0:T(8,128)(2,1)S(1)}, bf16[512,4096]{1,0:T(8,128)(2,1)}, u32[]{:S(2)}) copy-start(bf16[512,4096]{1,0:T(8,128)(2,1)} %param.32) | copy-start | bytes 12582916
  92.0 2.2 copy-start.6
  92.0 2.2 copy-start.5
  93.9 126.6 %all-reduce.6.cloned.1.call-start = ((), (), s32[]{:S(2)}) async-start(), calls=%async_computation.1 | async-start | bytes 2097152 | tf_op jit(solution)/shard_map/psum | solution.py:44
  160.2 4.9 %copy-start.4 = (bf16[512,4096]{1,0:T(8,128)(2,1)S(1)}, bf16[512,4096]{1,0:T(8,128)(2,1)}, u32[]{:S(2)}) copy-start(bf16[512,4096]{1,0:T(8,128)(2,1)} %param.34) | copy-start | bytes 12582916
  164.9 2.0 copy-start.7
  164.9 55.6 %copy-start.1 = (bf16[128,4096]{1,0:T(8,128)(2,1)S(1)}, bf16[128,4096]{1,0:T(8,128)(2,1)}, u32[]{:S(2)}) copy-start(bf16[128,4096]{1,0:T(8,128)(2,1)} %all-reduce.4.cloned.1.call-done) | copy-start | bytes 3145732
  166.9 136.8 %all-reduce.8.cloned.1.call-start = ((), (), s32[]{:S(2)}) async-start(), calls=%async_computation.2 | async-start | bytes 2097152 | tf_op jit(solution)/shard_map/psum | solution.py:44
Sparse Core Ops, SparseCore 0:
  94.1 55.1 all-reduce.3
  167.0 53.5 all-reduce.5
  250.2 53.5 all-reduce.7
where the time goes:
time: 316 us; the launch traced here: 313 us
  waiting for transfers between devices  162 us (51%)
  matrix products  59 us (19%)
  other arithmetic  40.5 us (13%)
  local copies, waits for them, and re-layouts  37 us (12%)
  between operations  14.1 us (4%)
    psum x3, waiting for transfers between devices, tp_sum(): return lax.psum(partial_out.astype(jnp.bfloat16), 'tp').astype(jnp.float32)  162 us
    gather x1, local copies, waits for them, and re-layouts, self_terms(): jnp.take(rel_bias, rel_bucket(distance), axis=0)  27.7 us
    select_n x1, other arithmetic, local_layer(): new_self_v = jnp.where(at_pos, new_values[:, None], self_v)  21.6 us
    dot_general x1, matrix products, local_layer(): jnp.dot(hidden, w_down, preferred_element_type=jnp.float32)  16.7 us
    dot_general x4, matrix products, project(): jnp.dot(normed, weight, preferred_element_type=jnp.float32)  12.5 us
    dot_general x2, matrix products, attend(): jnp.einsum('bht,bthk->bhk', probs_bf, values_all, preferred_element_type=...  9.46 us
    dot_general x1, matrix products, local_layer(): gate_pre = jnp.dot(normed, w_gate, preferred_element_type=jnp.float32)  9.08 us
    dot_general x2, matrix products, attend(): jnp.einsum('bhk,bthk->bht', queries, keys_all, preferred_element_type=jnp...  7.9 us
  transfers between devices with their start and end apart: 3, of which 3 were waited for; matrix products, arithmetic and copies ran while one was open for 0% of the time, Pallas kernels for 0%

commit v1 on v0

v1 whole, which is shorter than its diff:
```python
import functools
import math
import jax
import jax.numpy as jnp
from jax import lax
from jax.experimental import pallas as pl
from jax.experimental.pallas import tpu as pltpu
from jax.sharding import PartitionSpec as P

BUCKET_EDGES = tuple(int(math.ceil(16.0 * 8.0 ** (bucket_step / 16.0))) for bucket_step in range(1, 16))
NEG_FILL = -1e30
F32 = jnp.float32
BF16 = jnp.bfloat16
MESH = pl.DeviceIdType.MESH

CHUNKS = 4
POOL = 112


def lane_ids(rows):
    return lax.broadcasted_iota(jnp.int32, (rows, 256), 1)


def cache_copies(hbm, pool, base, first, count, sem, outward=False):
    for part in range(8):
        here = pool.at[pl.ds(base + first, count), pl.ds((part // 4) * 256, 256), pl.ds((part % 4) * 128, 128)]
        there = hbm.at[pl.ds(first, count), part]
        if outward:
            yield pltpu.make_async_copy(here, there, sem)
        else:
            yield pltpu.make_async_copy(there, here, sem)


def wait_slots(pool, base, count, sem):
    whole = pool.at[pl.ds(base, count)]
    pltpu.make_async_copy(whole, whole, sem).wait()


def put_columns(columns, refs):
    rows = columns.shape[0]
    for head in range(2):
        for half in range(2):
            at = (head * 2 + half) * 128
            refs[half][pl.ds(head, rows, stride=2), :] = columns[:, at:at + 128]


def scores_pass(q_refs, pool, base, first, last, w_ref):
    row_j = lax.rem(lax.broadcasted_iota(jnp.int32, (16, 128), 0), 8) // 2
    low = lax.rem(lane_ids(8) // 2, 2) == 0

    def body(slot, carry):
        for half in range(2):
            rows = pl.ds(pl.multiple_of(slot * 16 + half * 8, 8), 8)
            both = jnp.concatenate([q_refs[0][rows, :], q_refs[1][rows, :]], axis=0)
            lhs = jnp.concatenate([jnp.where(row_j == j, both, 0.0) for j in range(4)], axis=1).astype(BF16)
            keys = pool[base + slot, half * 256:half * 256 + 256, :]
            out = lax.dot_general(lhs, keys, (((1,), (1,)), ((), ())), preferred_element_type=F32)
            w_ref[rows, :] = jnp.where(low, out[:8], out[8:])
        return carry

    lax.fori_loop(first, last, body, 0, unroll=2)


def softmax_pass(w_ref, extra_ref, p_ref, rows_total):
    step = 64
    low = lax.rem(lane_ids(step) // 2, 2) == 0

    def body(index, carry):
        rows = pl.ds(pl.multiple_of(index * step, step), step)
        w = w_ref[rows, :]
        total = w + jnp.where(low, pltpu.roll(w, 254, 1), pltpu.roll(w, 2, 1)) + extra_ref[rows, :]
        e = jnp.exp(total - jnp.max(total, axis=1, keepdims=True))
        p_ref[rows, :] = e / (0.5 * jnp.sum(e, axis=1, keepdims=True))
        return carry

    lax.fori_loop(0, rows_total // step, body, 0)


def values_pass(p_ref, pool, base, first, last, o_refs):
    row_j = lax.broadcasted_iota(jnp.int32, (8, 128), 0) // 2
    low = lax.rem(lane_ids(8) // 2, 2) == 0

    def body(slot, carry):
        for half in range(2):
            rows = pl.ds(pl.multiple_of(slot * 16 + half * 8, 8), 8)
            p = p_ref[rows, :]
            lhs = jnp.concatenate([jnp.where(low, p, 0.0), jnp.where(low, 0.0, p)], axis=0).astype(BF16)
            vals = pool[base + slot, half * 256:half * 256 + 256, :]
            out = jnp.dot(lhs, vals, preferred_element_type=F32)
            for col_half in range(2):
                acc = jnp.zeros((8, 128), F32)
                for j in range(4):
                    acc = jnp.where(row_j == j, out[col_half * 8:col_half * 8 + 8, j * 128:j * 128 + 128], acc)
                o_refs[col_half][rows, :] = acc
        return carry

    lax.fori_loop(first, last, body, 0, unroll=2)


def get_mixed(o_refs, rows, head, half):
    return o_refs[half][pl.ds(head, rows, stride=2), :].astype(BF16)


def per_row(column, ref):
    rows = column.shape[0]
    for head in range(2):
        ref[pl.ds(head, rows, stride=2), :] = column


def self_kernel(x_hbm, tok_ref, tok_row, k_hbm, v_hbm, bias_ref, wq_hbm, wk_hbm, wv_hbm, norm_ref,
                mixed_ref, nk_hbm, nv_hbm,
                x_buf, h_buf, wq, wk, wv, pool, q0, q1, nk, nv, w_ref, p_ref, extra, o0, o1, pos_ref,
                x_sem, w_sem, in_sem, out_sem):
    rows = x_buf.shape[0]
    slots = rows // 8
    groups = in_sem.shape[1]
    per = slots // groups
    x_copy = pltpu.make_async_copy(x_hbm, x_buf, x_sem)
    x_copy.start()
    w_copies = [pltpu.make_async_copy(src, dst, w_sem.at[i]) for i, (src, dst) in enumerate(((wq_hbm, wq), (wk_hbm, wk), (wv_hbm, wv)))]
    for copy in w_copies:
        copy.start()
    for which, hbm in enumerate((k_hbm, v_hbm)):
        for group in range(groups):
            for copy in cache_copies(hbm, pool, which * slots, group * per, per, in_sem.at[which, group]):
                copy.start()

    tok = jnp.broadcast_to(tok_row[...].astype(F32), (rows, rows))
    per_row(tok.T, pos_ref)

    def extra_body(index, carry):
        at = pl.ds(pl.multiple_of(index * 32, 32), 32)
        lane = lane_ids(32)
        head = lax.rem(lax.broadcasted_iota(jnp.int32, (32, 256), 0), 2)
        pos = pos_ref[at, :]
        n = jnp.concatenate([pos, pos], axis=1) - (lane // 4).astype(F32)
        bias = jnp.where(head == 0, bias_ref[0, 0], bias_ref[0, 1])
        for bucket in range(1, 32):
            edge = bucket if bucket <= 16 else BUCKET_EDGES[bucket - 17]
            if edge > nk_hbm.shape[2] // 4 - 1:
                break
            bias = jnp.where(n >= float(edge), jnp.where(head == 0, bias_ref[bucket, 0], bias_ref[bucket, 1]), bias)
        keep = jnp.logical_and(n >= 0.0, lax.rem(lane, 2) == head)
        extra[at, :] = jnp.where(keep, bias, NEG_FILL)
        return carry

    lax.fori_loop(0, 2 * rows // 32, extra_body, 0)

    x_copy.wait()

    def norm_body(index, carry):
        at = pl.ds(pl.multiple_of(index * 16, 16), 16)
        values = x_buf[at, :].astype(F32)
        inv = lax.rsqrt(jnp.mean(values * values, axis=-1, keepdims=True) + 1e-6)
        h_buf[at, :] = (values * inv * norm_ref[...].astype(F32)).astype(BF16)
        return carry

    lax.fori_loop(0, rows // 16, norm_body, 0)

    def project(weight):
        return jnp.dot(h_buf[...], weight[...], preferred_element_type=F32).astype(BF16).astype(F32)

    w_copies[0].wait()
    put_columns(project(wq), (q0, q1))
    for copy, weight, ref in ((w_copies[1], wk, nk), (w_copies[2], wv, nv)):
        copy.wait()
        columns = project(weight)
        for head in range(2):
            for half in range(2):
                at = (head * 2 + half) * 128
                for rep in range(2):
                    ref[pl.ds(rep * 4 + half * 2 + head, rows, stride=8), :] = columns[:, at:at + 128]

    row_t = lax.broadcasted_iota(jnp.int32, (16, 128), 0) // 4

    def update(base, ref, first, last):
        def body(slot, carry):
            for half in range(2):
                for j in range(4):
                    row = slot * 8 + half * 4 + j
                    p = tok_ref[row]
                    at = pl.ds(pl.multiple_of(half * 256 + (p // 4) * 16, 16), 16)
                    old = pool[base + slot, at, j * 128:j * 128 + 128].astype(F32)
                    new = ref[pl.ds(pl.multiple_of(row * 8, 8), 8), :]
                    new = jnp.concatenate([new, new], axis=0)
                    pool[base + slot, at, j * 128:j * 128 + 128] = jnp.where(row_t == lax.rem(p, 4), new, old).astype(BF16)
            return carry

        lax.fori_loop(first, last, body, 0)

    for group in range(groups):
        first = group * per
        wait_slots(pool, first, per, in_sem.at[0, group])
        update(0, nk, first, first + per)
        for copy in cache_copies(nk_hbm, pool, 0, first, per, out_sem.at[0, group], True):
            copy.start()
        scores_pass((q0, q1), pool, 0, first, first + per, w_ref)
    softmax_pass(w_ref, extra, p_ref, 2 * rows)
    for group in range(groups):
        first = group * per
        wait_slots(pool, slots + first, per, in_sem.at[1, group])
        update(slots, nv, first, first + per)
        for copy in cache_copies(nv_hbm, pool, slots, first, per, out_sem.at[1, group], True):
            copy.start()
        values_pass(p_ref, pool, slots, first, first + per, (o0, o1))
    for head in range(2):
        for half in range(2):
            at = (head * 2 + half) * 128
            mixed_ref[:, at:at + 128] = get_mixed((o0, o1), rows, head, half)
    for which in range(2):
        for group in range(groups):
            wait_slots(pool, which * slots + group * per, per, out_sem.at[which, group])


def rest_kernel(chips, x_hbm, mixed_ref, mask_ref, k_hbm, v_hbm, wo_hbm, cq_hbm, co_hbm, wg_hbm, wu_hbm, wd_hbm,
                norm_cross, norm_mlp, out_hbm,
                pool, h_buf, part, r0, s1, r1, s2, r2, res, x_own, hidden, q0, q1, w_ref, p_ref, extra, o0, o1, len_ref, mixed2,
                x_sem, pool_sem, out_sem, rs_send, rs_recv, ag_send, ag_recv):
    rows = mask_ref.shape[0]
    slots = rows // 8
    chunks, _, width = h_buf.shape
    block = x_own.shape[0]
    half_rows = block * chips
    me = lax.axis_index("tp")
    core = lax.rem(me, 2)
    chip = me // 2
    flip1 = chip + 1 - 2 * lax.rem(chip, 2)
    flip3 = chips - 1 - chip
    near1 = flip1 + core * (flip3 - flip1)
    near2 = flip3 + core * (flip1 - flip3)
    far = lax.rem(chip + 2, chips)
    peer = me + 1 - 2 * core

    def device(chip_index):
        return {"tp": chip_index * 2 + core}

    at_wo, at_cq, at_k, at_v, at_co, at_gu = 0, 8, 16, 16 + slots, 16 + 2 * slots, 24 + 2 * slots
    at_d = at_gu + 64

    def slot_of(item):
        return lax.rem(item, POOL) if not isinstance(item, int) else item % POOL

    sem_count = [0]
    waits = {}

    def load(item, src, count):
        sem = pool_sem.at[sem_count[0]]
        sem_count[0] += 1
        base = slot_of(item)
        waits[item] = (base, count, sem)
        pltpu.make_async_copy(src, pool.at[pl.ds(base, count)], sem).start()

    def load_cache(item, hbm):
        sem = pool_sem.at[sem_count[0]]
        sem_count[0] += 1
        waits[item] = (item, slots, sem)
        for copy in cache_copies(hbm, pool, item, 0, slots, sem):
            copy.start()

    def ready(item):
        base, count, sem = waits.pop(item)
        wait_slots(pool, base, count, sem)

    x_copy = pltpu.make_async_copy(x_hbm.at[pl.ds(pl.multiple_of((core * chips + chip) * block, block), block)], x_own, x_sem)
    x_copy.start()
    for n in range(8):
        load(at_wo + n, wo_hbm.at[:, :, pl.ds(n * 512, 512)], 1)
    load(at_cq, cq_hbm, 8)

    barrier = pltpu.get_barrier_semaphore()
    for other in ({"tp": peer}, device(near1), device(near2)):
        pl.semaphore_signal(barrier, inc=1, device_id=other, device_id_type=MESH)

    lens = jnp.sum(mask_ref[...].astype(F32), axis=1, keepdims=True)
    per_row(jnp.broadcast_to(lens, (rows, 128)), len_ref)

    def extra_body(index, carry):
        at = pl.ds(pl.multiple_of(index * 32, 32), 32)
        lane = lane_ids(32)
        head = lax.rem(lax.broadcasted_iota(jnp.int32, (32, 256), 0), 2)
        length = len_ref[at, :]
        inside = (lane // 4).astype(F32) < jnp.concatenate([length, length], axis=1)
        extra[at, :] = jnp.where(jnp.logical_and(inside, lax.rem(lane, 2) == head), 0.0, NEG_FILL)
        return carry

    lax.fori_loop(0, 2 * rows // 32, extra_body, 0)
    pl.semaphore_wait(barrier, 3)

    load_cache(at_k, k_hbm)
    load_cache(at_v, v_hbm)
    for n in range(8):
        load(at_co + n, co_hbm.at[:, :, pl.ds(n * 512, 512)], 1)
    gate_up = [(at_gu + 16 * (i // 2) + 8 * (i % 2), (wg_hbm, wu_hbm)[i % 2].at[:, :, pl.ds((i // 2) * 512, 512)], 8) for i in range(8)]
    down = [(at_d + 4 * n, wd_hbm.at[:, :, pl.ds(n * 512, 512)], 4) for n in range(8)]
    later = [entry for entry in gate_up + down if entry[0] + entry[2] > POOL]
    for entry in gate_up + down:
        if entry[0] + entry[2] <= POOL:
            load(*entry)

    def load_freed(limit):
        while later and slot_of(later[0][0]) + later[0][2] <= limit:
            load(*later.pop(0))

    def remote(src, dst, sends, recvs, index, target):
        return pltpu.make_async_remote_copy(src_ref=src, dst_ref=dst, send_sem=sends.at[index], recv_sem=recvs.at[index],
                                            device_id=target, device_id_type=MESH)

    def rows_of(first):
        return pl.ds(pl.multiple_of(first, block), block)

    per_chunk = width // 512

    def all_sum(make, finish):
        pending = []
        stage0 = []
        for c in range(chunks):
            for i in range(per_chunk):
                part[c, :, i * 512:i * 512 + 512] = make(c * per_chunk + i).astype(BF16)
            copy = remote(part.at[c, pl.ds(pl.multiple_of((1 - core) * half_rows, half_rows), half_rows)], r0.at[c], rs_send, rs_recv, c, {"tp": peer})
            copy.start()
            stage0.append(copy)
        stage1 = []

        def chip_sum(c, which):
            mine = part[c, rows_of(core * half_rows + which * block), :].astype(F32)
            return mine + r0[c, rows_of(which * block), :].astype(F32)

        for c in range(chunks):
            stage0[c].wait_recv()
            s1[c, 0] = chip_sum(c, near1).astype(BF16)
            s1[c, 1] = chip_sum(c, far).astype(BF16)
            copy = remote(s1.at[c], r1.at[c], rs_send, rs_recv, chunks + c, device(near1))
            copy.start()
            stage1.append(copy)
        stage2 = []
        for c in range(chunks):
            stage1[c].wait_recv()
            s2[c] = (chip_sum(c, near2) + r1[c, 1].astype(F32)).astype(BF16)
            copy = remote(s2.at[c], r2.at[c], rs_send, rs_recv, 2 * chunks + c, device(near2))
            copy.start()
            stage2.append(copy)
        for c in range(chunks):
            stage2[c].wait_recv()
            res[c] = res[c] + (chip_sum(c, chip) + r1[c, 0].astype(F32) + r2[c].astype(F32))
        for copy in stage0 + stage1 + stage2:
            copy.wait_send()

        finish_chunk = finish()

        def rows_for(core_index, chip_index):
            return rows_of((core_index * chips + chip_index) * block)

        def send(c, chip_index, kind, target):
            where = h_buf.at[c, rows_for(core, chip_index)]
            copy = remote(where, where, ag_send, ag_recv, kind * chunks + c, target)
            copy.start()
            pending.append(copy)

        def arrived(c, kind, row_slice):
            where = h_buf.at[c, row_slice]
            remote(where, where, ag_send, ag_recv, kind * chunks + c, {"tp": peer}).wait_recv()

        for c in range(chunks):
            h_buf[c, rows_for(core, chip), :] = finish_chunk(c)
            send(c, chip, 0, device(near2))
            send(c, chip, 1, device(near1))
            send(c, chip, 3, {"tp": peer})
        for c in range(chunks):
            arrived(c, 0, rows_for(core, near2))
            send(c, near2, 2, device(near1))
            send(c, near2, 4, {"tp": peer})
        for c in range(chunks):
            arrived(c, 1, rows_for(core, near1))
            send(c, near1, 5, {"tp": peer})
        for c in range(chunks):
            arrived(c, 2, rows_for(core, far))
            send(c, far, 6, {"tp": peer})
        other = 1 - core
        for c in range(chunks):
            arrived(c, 3, rows_for(other, chip))
            arrived(c, 4, rows_for(other, near1))
            arrived(c, 5, rows_for(other, near2))
            arrived(c, 6, rows_for(other, far))
        return pending

    def done(pending):
        for copy in pending:
            copy.wait_send()

    def normed(norm_ref):
        def finish():
            square = jnp.zeros((block, 1), F32)
            for c in range(chunks):
                square = square + jnp.sum(res[c] * res[c], axis=1, keepdims=True)
            inv = lax.rsqrt(square / float(chunks * width) + 1e-6)

            def chunk(c):
                return (res[c] * inv * norm_ref[:, c * width:c * width + width].astype(F32)).astype(BF16)

            return chunk

        return finish

    def plain():
        return lambda c: res[c].astype(BF16)

    def h_part(k):
        return h_buf[k // per_chunk, :, (k % per_chunk) * 512:(k % per_chunk) * 512 + 512]

    x_copy.wait()
    for c in range(chunks):
        res[c] = x_own[:, c * width:c * width + width].astype(F32)

    def make_wo(n):
        ready(at_wo + n)
        return jnp.dot(mixed_ref[...], pool[at_wo + n], preferred_element_type=F32)

    pending = all_sum(make_wo, normed(norm_cross))
    load_freed(8)

    ready(at_cq)
    queries = jnp.dot(h_part(0), pool[at_cq], preferred_element_type=F32)
    for k in range(1, 8):
        queries = queries + jnp.dot(h_part(k), pool[at_cq + k], preferred_element_type=F32)
    put_columns(queries.astype(BF16).astype(F32), (q0, q1))
    done(pending)
    load_freed(16)
    ready(at_k)
    scores_pass((q0, q1), pool, at_k, 0, slots, w_ref)
    load_freed(16 + slots)
    softmax_pass(w_ref, extra, p_ref, 2 * rows)
    ready(at_v)
    values_pass(p_ref, pool, at_v, 0, slots, (o0, o1))
    load_freed(16 + 2 * slots)
    for head in range(2):
        for half in range(2):
            at = (head * 2 + half) * 128
            mixed2[:, at:at + 128] = get_mixed((o0, o1), rows, head, half)

    def make_co(n):
        ready(at_co + n)
        return jnp.dot(mixed2[...], pool[at_co + n], preferred_element_type=F32)

    pending = all_sum(make_co, normed(norm_mlp))

    for n in range(4):
        ready(at_gu + 16 * n)
        ready(at_gu + 16 * n + 8)

    def mlp_body(n, carry):
        def product(first):
            acc = jnp.dot(h_part(0), pool[slot_of(first)], preferred_element_type=F32)
            for k in range(1, 8):
                acc = acc + jnp.dot(h_part(k), pool[slot_of(first + k)], preferred_element_type=F32)
            return acc

        gate = product(at_gu + 16 * n)
        up = product(at_gu + 16 * n + 8)
        hidden[n] = (jax.nn.gelu(gate, approximate=True) * up).astype(BF16)
        return carry

    lax.fori_loop(0, 4, mlp_body, 0)
    done(pending)

    def make_down(n):
        ready(at_d + 4 * n)
        base = slot_of(at_d + 4 * n)
        acc = jnp.dot(hidden[0], pool[base], preferred_element_type=F32)
        for k in range(1, 4):
            acc = acc + jnp.dot(hidden[k], pool[base + k], preferred_element_type=F32)
        return acc

    pending = all_sum(make_down, plain)
    copies = [pltpu.make_async_copy(h_buf.at[c], out_hbm.at[:, pl.ds(c * width, width)], out_sem.at[c]) for c in range(chunks)]
    for copy in copies:
        copy.start()
    done(pending)
    for copy in copies:
        copy.wait()


def solution(mesh):
    chips = mesh.shape["tp"] // 2
    any_space = pl.BlockSpec(memory_space=pl.ANY)
    vmem = pl.BlockSpec(memory_space=pltpu.VMEM)
    smem = pl.BlockSpec(memory_space=pltpu.SMEM)

    def local_layer(x_in, tok_pos, self_k, self_v, cross_k, cross_v, enc_mask, rel_bias, w_q, w_k, w_v, w_o, cross_q, cross_o, w_gate, w_up, w_down, norm_self, norm_cross, norm_mlp):
        rows, t_len, heads, dim = self_k.shape
        model = x_in.shape[1]
        slots = rows // 8
        flat = heads * dim

        def packed(cache):
            return cache.reshape(rows, t_len, heads, 2, 128).transpose(0, 1, 3, 2, 4).reshape(slots, 8, t_len * 4, 128)

        def unpacked(cache):
            return cache.reshape(rows, t_len, 2, heads, 128).transpose(0, 1, 3, 2, 4).reshape(rows, t_len, heads, dim)

        cache_shape = jax.ShapeDtypeStruct((slots, 8, t_len * 4, 128), BF16)
        groups = 4
        work = [pltpu.VMEM((2 * rows, 256), F32)] * 3 + [pltpu.VMEM((2 * rows, 128), F32)] * 3
        mixed, new_k, new_v = pl.pallas_call(
            self_kernel,
            name="self_attention",
            out_shape=(jax.ShapeDtypeStruct((rows, flat), BF16), cache_shape, cache_shape),
            in_specs=[any_space, smem, vmem, any_space, any_space, smem, any_space, any_space, any_space, vmem],
            out_specs=(vmem, any_space, any_space),
            scratch_shapes=[
                pltpu.VMEM((rows, model), BF16), pltpu.VMEM((rows, model), BF16),
                pltpu.VMEM((model, flat), BF16), pltpu.VMEM((model, flat), BF16), pltpu.VMEM((model, flat), BF16),
                pltpu.VMEM((2 * slots, 512, 512), BF16),
                pltpu.VMEM((2 * rows, 128), F32), pltpu.VMEM((2 * rows, 128), F32),
                pltpu.VMEM((8 * rows, 128), F32), pltpu.VMEM((8 * rows, 128), F32),
                *work,
                pltpu.SemaphoreType.DMA, pltpu.SemaphoreType.DMA((3,)),
                pltpu.SemaphoreType.DMA((2, groups)), pltpu.SemaphoreType.DMA((2, groups)),
            ],
            compiler_params=pltpu.CompilerParams(vmem_limit_bytes=63 << 20),
        )(x_in, tok_pos, tok_pos.reshape(1, rows), packed(self_k), packed(self_v), rel_bias, w_q, w_k, w_v, norm_self.reshape(1, model))

        width = model // CHUNKS
        block = rows // (2 * chips)
        x_out = pl.pallas_call(
            functools.partial(rest_kernel, chips),
            name="rest_of_layer",
            out_shape=jax.ShapeDtypeStruct((rows, model), BF16),
            in_specs=[any_space, vmem, vmem] + [any_space] * 8 + [vmem, vmem],
            out_specs=any_space,
            scratch_shapes=[
                pltpu.VMEM((POOL, 512, 512), BF16),
                pltpu.VMEM((CHUNKS, rows, width), BF16), pltpu.VMEM((CHUNKS, rows, width), BF16),
                pltpu.VMEM((CHUNKS, rows // 2, width), BF16),
                pltpu.VMEM((CHUNKS, 2, block, width), BF16), pltpu.VMEM((CHUNKS, 2, block, width), BF16),
                pltpu.VMEM((CHUNKS, block, width), BF16), pltpu.VMEM((CHUNKS, block, width), BF16),
                pltpu.VMEM((CHUNKS, block, width), F32), pltpu.VMEM((block, model), BF16),
                pltpu.VMEM((4, rows, 512), BF16),
                pltpu.VMEM((2 * rows, 128), F32), pltpu.VMEM((2 * rows, 128), F32),
                *work,
                pltpu.VMEM((rows, flat), BF16),
                pltpu.SemaphoreType.DMA, pltpu.SemaphoreType.DMA((40,)), pltpu.SemaphoreType.DMA((CHUNKS,)),
                pltpu.SemaphoreType.DMA((3 * CHUNKS,)), pltpu.SemaphoreType.DMA((3 * CHUNKS,)),
                pltpu.SemaphoreType.DMA((7 * CHUNKS,)), pltpu.SemaphoreType.DMA((7 * CHUNKS,)),
            ],
            compiler_params=pltpu.CompilerParams(collective_id=0, has_side_effects=True, vmem_limit_bytes=67_043_328),
        )(x_in, mixed, enc_mask, packed(cross_k), packed(cross_v), w_o.reshape(1, flat, model), cross_q.reshape(8, model // 8, flat),
          cross_o.reshape(1, flat, model), w_gate.reshape(8, model // 8, -1), w_up.reshape(8, model // 8, -1), w_down.reshape(4, -1, model),
          norm_cross.reshape(1, model), norm_mlp.reshape(1, model))
        return x_out, unpacked(new_k), unpacked(new_v)

    cache_spec = P('dp', None, 'tp', None)
    split_cols = P(None, 'tp')
    split_rows = P('tp', None)
    in_specs = (P('dp', None), P('dp'), cache_spec, cache_spec, cache_spec, cache_spec, P('dp', None), split_cols, split_cols, split_cols, split_cols, split_rows, split_cols, split_rows, split_cols, split_cols, split_rows, P(None), P(None), P(None))
    out_specs = (P('dp', None), cache_spec, cache_spec)
    return jax.shard_map(local_layer, mesh=mesh, in_specs=in_specs, out_specs=out_specs, check_vma=False)
```

time: 316 us -> 110 us (0.35)
  the two profiles are of different devices: /device:TPU:113 before, /device:TPU:125 now
where the time goes in v1:
time: 110 us
  Pallas kernels  100 us (91%)
  local copies, waits for them, and re-layouts  9.05 us (8%)
    pallas_call x1, Pallas kernels, local_layer(): pl.pallas_call(functools.partial(rest_kernel, chips), name='rest_of_layer...  81.8 us
    pallas_call x1, Pallas kernels, local_layer(): pl.pallas_call(self_kernel, name='self_attention', out_shape=(jax.ShapeDt...  18.1 us
    unnamed x3, local copies, waits for them, and re-layouts  5.13 us

profile of v1, /device:TPU:125, one launch (start us, length us, event | category | flops | bytes accessed | tf_op | source)
XLA Modules:
  0.0 109.7 jit_solution(16264967924555359017)
XLA Ops:
  0.6 1.4 %copy.25.bias_ref = f32[32,2]{1,0:T(8,128)} copy(f32[32,2]{0,1:T(2,128)} %param.27) | data formatting | bytes 512 | tf_op args[7]
  2.0 1.3 %reshape.77.norm_ref = bf16[1,4096]{1,0:T(2,128)(2,1)} reshape(bf16[4096]{0:T(1024)(128)(2,1)} %param.37) | data formatting | bytes 16384 | tf_op jit(solution)/shard_map/reshape | solution.py:520
  3.3 1.3 %reshape.88.norm_cross = bf16[1,4096]{1,0:T(2,128)(2,1)} reshape(bf16[4096]{0:T(1024)(128)(2,1)} %param.38) | data formatting | bytes 16384 | tf_op jit(solution)/shard_map/reshape | solution.py:548
  4.6 1.3 %reshape.89.norm_mlp = bf16[1,4096]{1,0:T(2,128)(2,1)} reshape(bf16[4096]{0:T(1024)(128)(2,1)} %param.39) | data formatting | bytes 16384 | tf_op jit(solution)/shard_map/reshape | solution.py:548
  5.9 1.5 %copy.28.mask_ref = s32[128,64]{1,0:T(8,128)} copy(s32[128,64]{0,1:T(8,128)} %param.26) | data formatting | bytes 65536 | tf_op args[6]
  7.4 18.1 %self_attention.1 = (bf16[128,512]{1,0:T(8,128)(2,1)}, bf16[16,8,256,128]{3,2,1,0:T(8,128)(2,1)}, bf16[16,8,256,128]{3,2,1,0:T(8,128)(2,1)}) custom-call(bf16[128,4096]{1,0:T(8,128)(2,1)} %x_hbm.3, s32[128]{0:T(128)} %tok_ref.1, s32[1,128]{1,0:T(1,128)} %bitcast.47, bf16[16,8,256,128]{3,2,1,0:T(8,128)(2,1)} %bitcast.40, bf16[16,8,256,128]{3,2,1,0:T(8,128)(2,1)} %bitcast.41, ...), custom_call_target="tpu_custom_call" | custom-call | tf_op jit(solution)/shard_map/self_attention/pallas_call | solution.py:503
  25.5 81.8 %rest_of_layer.1 = bf16[128,4096]{1,0:T(8,128)(2,1)} custom-call(bf16[128,4096]{1,0:T(8,128)(2,1)} %x_hbm.3, bf16[128,512]{1,0:T(8,128)(2,1)} %get-tuple-element.6.mixed_ref, s32[128,64]{1,0:T(8,128)} %copy.28.mask_ref, bf16[16,8,256,128]{3,2,1,0:T(8,128)(2,1)} %bitcast.42, bf16[16,8,256,128]{3,2,1,0:T(8,128)(2,1)} %bitcast.43, ...), custom_call_target="tpu_custom_call" | custom-call | tf_op jit(solution)/shard_map/rest_of_layer/pallas_call | solution.py:524
  107.4 2.3 %copy.32 = bf16[128,4096]{1,0:T(8,128)(2,1)} copy(bf16[128,4096]{1,0:T(8,128)(2,1)} %rest_of_layer.1) | data formatting | bytes 2097152
